TPU v7x, 32 devices: a whole 2x2x4 slice. The times are simulated.
32 devices in a mesh: rep: 2 (over y), own: 16 (over z, x, core).
Axes of the slice: x: 2, y: 2, z: 4, core: 2. Of those that a mesh axis runs over, the one named last changes fastest.
Arguments:
- values: float32 [262144, 128], P(('rep', 'own')), may hold values from -0.8 to 0.8
- key_ids: int32 [262144], P(('rep', 'own')), may hold values from 0 to 65535, as said below
- heavy_ids: int32 [2048], replicated, may hold values from 0 to 65535, as said below
- block_offsets: int32 [32, 16], P(('rep', 'own')), may hold values from 0 to 8191, as said below
- block_counts: int32 [32, 16], P(('rep', 'own')), may hold values from 8 to 64, as said below
Outputs:
- light_sums: float32 [65536, 128], P('own')
- heavy_sums: float32 [2048, 128], P('own')
Inputs may be any that keep to these rules, and one draw needn't show every extreme that they name: `key_ids`: an event in block o of a device has a key in o * 4096 to (o + 1) * 4096 - 1 that is not a heavy key; every event outside all blocks has a heavy key. `heavy_ids`: distinct keys. `block_offsets`: on each device the blocks lie in the order of o, do not meet, and end by position 8192. `block_counts`: at most 64; one owner gets exactly 64 from every device.
All inputs are finite; a program needn't handle non-finite values.
Results may differ from a plain program's by a relative error of at most 0.000075.
Values sent between devices are 32-bit elements; how exact they have to be, the bound alone decides.
A program may use at most 64 MiB of HBM per device.

v0:
```python
import math
import jax
import jax.numpy as jnp
from jax import lax
from jax.sharding import PartitionSpec as P

KEYS_DEV = 4096
CAP = 64


def key_sums(rows_in, row_keys, targets):
    slots = row_keys.shape[0]
    block_len = math.gcd(slots, 2048)
    count_blocks = slots // block_len
    rows_blocks = rows_in.reshape(count_blocks, block_len, rows_in.shape[1])
    keys_blocks = row_keys.reshape(count_blocks, block_len)

    def accumulate(running, pieces):
        rows_piece, keys_piece = pieces
        onehot = (targets[:, None] == keys_piece[None, :]).astype(jnp.float32)
        added = jnp.dot(
            onehot, rows_piece, precision=lax.Precision.HIGHEST, preferred_element_type=jnp.float32
        )
        return (running + added, None)

    start_sums = jnp.zeros((targets.shape[0], rows_in.shape[1]), jnp.float32)
    running, unused = lax.scan(accumulate, start_sums, (rows_blocks, keys_blocks))
    return running


def per_device(values, key_ids, heavy_ids, block_offsets, block_counts):
    owners = lax.axis_size("own")
    pairs = lax.axis_size("rep")
    own_index = lax.axis_index("own")
    rep_index = lax.axis_index("rep")
    width = values.shape[1]
    slot_cap = CAP
    padded_values = jnp.concatenate([values, jnp.zeros((slot_cap, width), jnp.float32)], axis=0)
    padded_keys = jnp.concatenate([key_ids, jnp.full((slot_cap,), -1, jnp.int32)], axis=0)
    slot_iota = jnp.arange(slot_cap, dtype=jnp.int32)
    positions = block_offsets[0][:, None] + slot_iota[None, :]
    valid = slot_iota[None, :] < block_counts[0][:, None]
    block_rows = jnp.where(valid[:, :, None], jnp.take(padded_values, positions, axis=0), 0.0)
    block_keys = jnp.where(valid, jnp.take(padded_keys, positions, axis=0), -1)
    half_keys = KEYS_DEV // 2
    owner_base = (jnp.arange(owners, dtype=jnp.int32) * KEYS_DEV)[:, None]
    which_half = jnp.where(block_keys >= 0, (block_keys - owner_base) // half_keys, -1)
    split_rows = jnp.stack(
        [jnp.where((which_half == side)[:, :, None], block_rows, 0.0) for side in range(pairs)],
        axis=0,
    )
    split_keys = jnp.stack(
        [jnp.where(which_half == side, block_keys, -1) for side in range(pairs)], axis=0
    )
    split_rows = split_rows.reshape(pairs * owners, slot_cap, width)
    split_keys = split_keys.reshape(pairs * owners, slot_cap)
    got_rows, got_keys = (
        lax.all_to_all(split_rows, ("rep", "own"), split_axis=0, concat_axis=0, tiled=True),
        lax.all_to_all(split_keys, ("rep", "own"), split_axis=0, concat_axis=0, tiled=True),
    )
    local_keys = jnp.where(
        got_keys >= 0, got_keys - own_index * KEYS_DEV - rep_index * half_keys, -1
    ).reshape(-1)
    owned_half = key_sums(
        got_rows.reshape(-1, width), local_keys, jnp.arange(half_keys, dtype=jnp.int32)
    )
    light_sums = lax.all_gather(owned_half, "rep", axis=0, tiled=True)
    partial_sums = key_sums(values, key_ids, heavy_ids)
    summed_pair = lax.psum(partial_sums, "rep")
    heavy_sums = lax.psum_scatter(summed_pair, "own", scatter_dimension=0, tiled=True)
    return (light_sums, heavy_sums)


def solution(mesh):
    placed = (
        P(("rep", "own"), None),
        P(("rep", "own")),
        P(),
        P(("rep", "own"), None),
        P(("rep", "own"), None),
    )
    return jax.shard_map(
        per_device,
        mesh=mesh,
        in_specs=placed,
        out_specs=(P("own", None), P("own", None)),
        check_vma=False,
    )
```

profile of v0, /device:TPU:0, one launch (start us, length us, event | category | flops | bytes accessed | tf_op | source)
XLA Modules:
  0.0 166.0 jit_solution(6468750620577032743)
XLA Ops:
  8.0 0.7 compare_select_fusion.2
  8.7 0.1 reshape.548
  8.8 0.8 concatenate.6
  9.6 0.0 copy-start.3
  9.6 0.0 copy-start.4
  9.6 6.1 %gather_fusion = s32[1024]{0:T(1024)S(1)} fusion(s32[8256]{0:T(1024)S(1)} %concatenate.6, s32[1024]{0:T(1024)S(1)} %broadcast_clamp_fusion), kind=kCustom, calls=%fused_computation | custom fusion | bytes 12288 | tf_op jit(solution)/shard_map/jit(_take)/gather | solution.py:44
  15.7 0.1 gather.13
  15.8 0.0 copy-done.3
  15.8 0.0 copy-done.4
  15.8 0.1 compare_select_fusion.5
  15.9 0.6 pad_add_fusion
  16.5 7.3 %all-to-all-start = ((s32[32,1,64]{2,1,0:T(1,128)}), s32[32,1,64]{2,1,0:T(1,128)S(1)}, u32[]{:S(2)}, u32[]{:S(2)}) async-start(s32[32,1,64]{2,1,0:T(1,128)} %bitcast.2), calls=%async_computation | async-start | bytes 32768 | tf_op jit(solution)/shard_map/all_to_all | solution.py:59
  23.8 0.1 reshape.547
  23.9 3.7 %concatenate.7 = f32[8256,128]{1,0:T(8,128)} pad(f32[8192,128]{1,0:T(8,128)} %param.7, f32[]{:T(128)} %constant.82.clone.1), padding=0_64x0_0 | pad | bytes 8421380 | tf_op jit(solution)/shard_map/concatenate | solution.py:38
  27.6 0.0 copy-start.1
  27.6 0.0 copy-start.5
  27.6 5.0 %gather_fusion.1 = f32[1024,128]{1,0:T(8,128)S(1)} fusion(f32[8256,128]{1,0:T(8,128)} %concatenate.7, s32[1024]{0:T(1024)S(1)} %broadcast_clamp_fusion), kind=kCustom, calls=%fused_computation.1 | custom fusion | bytes 1052672 | tf_op jit(solution)/shard_map/jit(_take)/gather | solution.py:43
  32.6 0.1 broadcast_compare_fusion.1
  32.8 0.7 fusion.13
  33.5 1.1 pad_maximum_fusion
  34.6 0.0 copy-done.1
  34.6 0.0 all-to-all-done
  34.6 5.8 %all-to-all-start.1 = ((f32[32,64,128]{2,1,0:T(8,128)}), f32[32,64,128]{2,1,0:T(8,128)S(1)}, u32[]{:S(2)}, u32[]{:S(2)}) async-start(f32[32,64,128]{2,1,0:T(8,128)} %bitcast.4), calls=%async_computation.1 | async-start | bytes 2097152 | tf_op jit(solution)/shard_map/all_to_all | solution.py:58
  40.4 0.0 reduce-scatter.2.cloned.1.call-start
  40.5 0.0 copy-done.5
  40.5 34.5 %while.3 = (s32[]{:T(128)}, f32[2048,128]{1,0:T(8,128)S(1)}, s32[2048]{0:T(1024)S(1)}, s32[4,2048]{1,0:T(4,128)S(1)}, f32[4,2048,128]{2,1,0:T(8,128)}, /*index=5*/s32[]{:T(128)}, s32[]{:T(128)}) while((s32[]{:T(128)}, f32[2048,128]{1,0:T(8,128)S(1)}, s32[2048]{0:T(1024)S(1)}, s32[4,2048]{1,0:T(4,128)S(1)}, ...), condition=%wide.region_1.2_spmd.clone, body=%wide.region_0.1_spmd.clone.sunk | while | flops 6447169536 | bytes 3178599 | solution.py:27
  40.5 8.6 %fusion.34 = f32[2048,128]{1,0:T(8,128)S(1)} fusion(s32[2048]{0:T(1024)S(1)} %bitcast.21, s32[2048]{0:T(1024)S(1)} %get-tuple-element.128, f32[2048,128]{1,0:T(8,128)S(1)} %get-tuple-element.120, f32[4,2048,128]{2,1,0:T(8,128)} %get-tuple-element.130, s32[]{:T(128)S(6)} %copy.9, pred[]{:T(512)S(6)} %compare.29), kind=kOutput, calls=%fused_computation.6.clone.1 | convolution fusion | flops 6447169536 | bytes 3162117 | tf_op jit(solution)/shard_map/while/body/eval_jaxpr/dot_general | solution.py:21
  49.2 8.6 %fusion.34 = f32[2048,128]{1,0:T(8,128)S(1)} fusion(s32[2048]{0:T(1024)S(1)} %bitcast.21, s32[2048]{0:T(1024)S(1)} %get-tuple-element.128, f32[2048,128]{1,0:T(8,128)S(1)} %get-tuple-element.120, f32[4,2048,128]{2,1,0:T(8,128)} %get-tuple-element.130, s32[]{:T(128)S(6)} %copy.9, pred[]{:T(512)S(6)} %compare.29), kind=kOutput, calls=%fused_computation.6.clone.1 | convolution fusion | flops 6447169536 | bytes 3162117 | tf_op jit(solution)/shard_map/while/body/eval_jaxpr/dot_general | solution.py:21
  57.8 8.6 %fusion.34 = f32[2048,128]{1,0:T(8,128)S(1)} fusion(s32[2048]{0:T(1024)S(1)} %bitcast.21, s32[2048]{0:T(1024)S(1)} %get-tuple-element.128, f32[2048,128]{1,0:T(8,128)S(1)} %get-tuple-element.120, f32[4,2048,128]{2,1,0:T(8,128)} %get-tuple-element.130, s32[]{:T(128)S(6)} %copy.9, pred[]{:T(512)S(6)} %compare.29), kind=kOutput, calls=%fused_computation.6.clone.1 | convolution fusion | flops 6447169536 | bytes 3162117 | tf_op jit(solution)/shard_map/while/body/eval_jaxpr/dot_general | solution.py:21
  66.4 8.6 %fusion.34 = f32[2048,128]{1,0:T(8,128)S(1)} fusion(s32[2048]{0:T(1024)S(1)} %bitcast.21, s32[2048]{0:T(1024)S(1)} %get-tuple-element.128, f32[2048,128]{1,0:T(8,128)S(1)} %get-tuple-element.120, f32[4,2048,128]{2,1,0:T(8,128)} %get-tuple-element.130, s32[]{:T(128)S(6)} %copy.9, pred[]{:T(512)S(6)} %compare.29), kind=kOutput, calls=%fused_computation.6.clone.1 | convolution fusion | flops 6447169536 | bytes 3162117 | tf_op jit(solution)/shard_map/while/body/eval_jaxpr/dot_general | solution.py:21
  75.0 0.0 copy-start
  75.0 1.0 copy-done
  76.0 0.0 reduce-scatter.2.cloned.1.call-update
  76.0 0.2 all-gather.2.cloned.1.call-start
  76.2 0.1 fusion.14
  76.3 0.1 select_n.222
  76.4 0.0 all-to-all-done.1
  76.4 8.6 %fusion.10 = f32[2048,128]{1,0:T(8,128)} fusion(f32[2048,128]{1,0:T(8,128)S(1)} %bitcast.20, s32[2048]{0:T(1024)S(1)} %select_n.222), kind=kOutput, calls=%fused_computation.12 | convolution fusion | flops 6446645248 | bytes 2105344 | tf_op jit(solution)/shard_map/while/body/eval_jaxpr/dot_general | solution.py:21
  84.9 0.0 all-gather.2.cloned.1.call-update
  85.0 0.0 all-reduce.4.cloned.1.call-start
  85.0 50.0 %reduce-scatter.2.cloned.1.call-done = f32[128,128]{1,0:T(8,128)} async-done(((f32[2048,128]{1,0:T(8,128)}), f32[128,128]{1,0:T(8,128)}) %reduce-scatter.2.cloned.1.call-update) | async-done | bytes 65552 | tf_op jit(solution)/shard_map/reduce_scatter | solution.py:70
  135.0 0.0 all-reduce.4.cloned.1.call-update
  135.0 0.0 all-gather.2.cloned.1.call-done
  135.0 19.8 %all-reduce.4.cloned.1.call-done = f32[128,128]{1,0:T(8,128)} async-done(((f32[128,128]{1,0:T(8,128)}), f32[128,128]{1,0:T(8,128)}) %all-reduce.4.cloned.1.call-update) | async-done | bytes 65552 | tf_op jit(solution)/shard_map/psum | solution.py:69
  154.9 0.0 copy-start.2
  154.9 3.1 %copy.15 = f32[4096,128]{1,0:T(8,128)} copy(f32[4096,128]{1,0:T(8,128)} %all-gather.2.cloned.1.call-done) | data formatting | bytes 4194304
  157.9 0.0 copy-done.2
  157.9 0.6 copy.16
  (9 shorter events, 0.1 us)
Async XLA Ops:
  9.6 6.2 %copy-start.3 = (s32[1,16]{1,0:T(1,128)S(1)}, s32[1,16]{1,0:T(1,128)}, u32[]{:S(2)}) copy-start(s32[1,16]{1,0:T(1,128)} %param.10) | copy-start | bytes 196
  9.6 6.2 %copy-start.4 = (s32[1,16]{1,0:T(1,128)S(1)}, s32[1,16]{1,0:T(1,128)}, u32[]{:S(2)}) copy-start(s32[1,16]{1,0:T(1,128)} %param.11) | copy-start | bytes 196
  16.5 18.1 %all-to-all-start = ((s32[32,1,64]{2,1,0:T(1,128)}), s32[32,1,64]{2,1,0:T(1,128)S(1)}, u32[]{:S(2)}, u32[]{:S(2)}) async-start(s32[32,1,64]{2,1,0:T(1,128)} %bitcast.2), calls=%async_computation | async-start | bytes 32768 | tf_op jit(solution)/shard_map/all_to_all | solution.py:59
  27.6 6.9 %copy-start.1 = (s32[8192]{0:T(1024)S(1)}, s32[8192]{0:T(1024)}, u32[]{:S(2)}) copy-start(s32[8192]{0:T(1024)} %param.8) | copy-start | bytes 98308
  27.6 12.9 %copy-start.5 = (s32[2048]{0:T(1024)S(1)}, s32[2048]{0:T(1024)}, u32[]{:S(2)}) copy-start(s32[2048]{0:T(1024)} %param.9) | copy-start | bytes 24580
  34.6 41.8 %all-to-all-start.1 = ((f32[32,64,128]{2,1,0:T(8,128)}), f32[32,64,128]{2,1,0:T(8,128)S(1)}, u32[]{:S(2)}, u32[]{:S(2)}) async-start(f32[32,64,128]{2,1,0:T(8,128)} %bitcast.4), calls=%async_computation.1 | async-start | bytes 2097152 | tf_op jit(solution)/shard_map/all_to_all | solution.py:58
  40.4 94.5 %reduce-scatter.2.cloned.1.call-start = ((), (), s32[]{:S(2)}) async-start(), calls=%async_computation.4 | async-start | bytes 1114112 | tf_op jit(solution)/shard_map/reduce_scatter | solution.py:70
  75.0 1.0 copy-start
  76.0 59.1 %all-gather.2.cloned.1.call-start = ((), (), s32[]{:S(2)}) async-start(), calls=%async_computation.3 | async-start | bytes 3145728 | tf_op jit(solution)/shard_map/all_gather | solution.py:67
  85.0 69.9 %all-reduce.4.cloned.1.call-start = ((), (), s32[]{:S(2)}) async-start(), calls=%async_computation.5 | async-start | bytes 131072 | tf_op jit(solution)/shard_map/psum | solution.py:69
  154.9 3.1 %copy-start.2 = (f32[128,128]{1,0:T(8,128)S(1)}, f32[128,128]{1,0:T(8,128)}, u32[]{:S(2)}) copy-start(f32[128,128]{1,0:T(8,128)} %all-reduce.4.cloned.1.call-done) | copy-start | bytes 196612
Sparse Core Ops, SparseCore 0:
  76.1 58.8 reduce-scatter.1
Sparse Core Ops, SparseCore 1:
  85.0 34.2 all-gather.1
  135.1 19.7 all-reduce.3
where the time goes:
time: 167 us; the launch traced here: 166 us
  waiting for transfers between devices  69.9 us (42%)
  matrix products  42.9 us (26%)
  local copies, waits for them, and re-layouts  20.7 us (12%)
  between operations  15.6 us (9%)
  starting transfers between devices  13.5 us (8%)
  other arithmetic  3.39 us (2%)
    reduce_scatter x1, waiting for transfers between devices, per_device(): lax.psum_scatter(summed_pair, 'own', scatter_dimension=0, tiled=True)  50 us
    dot_general x5, matrix products, accumulate(): jnp.dot(onehot, rows_piece, precision=lax.Precision.HIGHEST, preferred_el...  42.9 us
    psum x1, waiting for transfers between devices, per_device(): summed_pair = lax.psum(partial_sums, 'rep')  19.8 us
    all_to_all x1, starting transfers between devices, per_device(): lax.all_to_all(split_keys, ('rep', 'own'), split_axis=0, concat_axis=0, t...  7.33 us
    gather x3, local copies, waits for them, and re-layouts, per_device(): block_keys = jnp.where(valid, jnp.take(padded_keys, positions, axis=0), -1)  6.28 us
    all_to_all x1, starting transfers between devices, per_device(): lax.all_to_all(split_rows, ('rep', 'own'), split_axis=0, concat_axis=0, t...  5.84 us
    gather x1, local copies, waits for them, and re-layouts, per_device(): jnp.take(padded_values, positions, axis=0)  5 us
    unnamed x14, local copies, waits for them, and re-layouts  4.68 us
  transfers between devices with their start and end apart: 5, of which 2 were waited for; matrix products, arithmetic and copies ran while one was open for 32% of the time, Pallas kernels for 0%

commit v1 on v0

--- a/solution.py
+++ b/solution.py
@@ -66,7 +66,7 @@
     )
     light_sums = lax.all_gather(owned_half, "rep", axis=0, tiled=True)
     partial_sums = key_sums(values, key_ids, heavy_ids)
-    summed_pair = lax.psum(partial_sums, "rep")
+    summed_pair = partial_sums + lax.ppermute(partial_sums, "rep", [(0, 1), (1, 0)])
     heavy_sums = lax.psum_scatter(summed_pair, "own", scatter_dimension=0, tiled=True)
     return (light_sums, heavy_sums)
 

time: 167 us -> 203 us (1.22)
  waiting for transfers between devices: 69.9 us -> 106 us
    all_to_all x1, waiting for transfers between devices: 0.01 us -> 26.9 us  [per_device(): lax.all_to_all(split_rows, ('rep', 'own'), split_axis=0, concat_axis=0, t...]
    ppermute x0 -> x1, waiting for transfers between devices: none -> 23.7 us  [per_device(): lax.ppermute(partial_sums, 'rep', [(0, 1), (1, 0)])]
    psum x1 -> x0, waiting for transfers between devices: 19.8 us -> none  [per_device(): summed_pair = lax.psum(partial_sums, 'rep')]
    reduce_scatter x1, waiting for transfers between devices: 50 us -> 55.3 us  [per_device(): lax.psum_scatter(summed_pair, 'own', scatter_dimension=0, tiled=True)]
    unnamed x14 -> x9, local copies, waits for them, and re-layouts: 4.68 us -> 3.06 us
  transfers between devices with their start and end apart: 5 -> 5, of which waited for: 2 -> 3; matrix products, arithmetic and copies ran while one was open for 32% -> 23% of each run, Pallas kernels for 0% -> 0%
where the time goes in v1:
time: 203 us; the launch traced here: 202 us
  waiting for transfers between devices  106 us (52%)
  matrix products  42.9 us (21%)
  local copies, waits for them, and re-layouts  19 us (9%)
  between operations  15.6 us (8%)
  starting transfers between devices  14.3 us (7%)
  other arithmetic  4.47 us (2%)
    reduce_scatter x1, waiting for transfers between devices, per_device(): lax.psum_scatter(summed_pair, 'own', scatter_dimension=0, tiled=True)  55.3 us
    dot_general x5, matrix products, accumulate(): jnp.dot(onehot, rows_piece, precision=lax.Precision.HIGHEST, preferred_el...  42.9 us
    all_to_all x1, waiting for transfers between devices, per_device(): lax.all_to_all(split_rows, ('rep', 'own'), split_axis=0, concat_axis=0, t...  26.9 us
    ppermute x1, waiting for transfers between devices, per_device(): lax.ppermute(partial_sums, 'rep', [(0, 1), (1, 0)])  23.7 us
    all_to_all x1, starting transfers between devices, per_device(): lax.all_to_all(split_keys, ('rep', 'own'), split_axis=0, concat_axis=0, t...  7.33 us
    gather x3, local copies, waits for them, and re-layouts, per_device(): block_keys = jnp.where(valid, jnp.take(padded_keys, positions, axis=0), -1)  6.28 us
    all_to_all x1, starting transfers between devices, per_device(): lax.all_to_all(split_rows, ('rep', 'own'), split_axis=0, concat_axis=0, t...  5.83 us
    gather x1, local copies, waits for them, and re-layouts, per_device(): jnp.take(padded_values, positions, axis=0)  5.01 us
  transfers between devices with their start and end apart: 5, of which 3 were waited for; matrix products, arithmetic and copies ran while one was open for 23% of the time, Pallas kernels for 0%

profile of v1, /device:TPU:0, one launch (start us, length us, event | category | flops | bytes accessed | tf_op | source)
XLA Modules:
  0.0 202.5 jit_solution(698761218617572069)
XLA Ops:
  8.0 0.7 compare_select_fusion.2
  8.7 0.1 reshape.548
  8.8 0.8 concatenate.6
  9.6 0.0 copy-start.1
  9.6 0.0 copy-start.2
  9.6 6.1 %gather_fusion = s32[1024]{0:T(1024)S(1)} fusion(s32[8256]{0:T(1024)S(1)} %concatenate.6, s32[1024]{0:T(1024)S(1)} %broadcast_clamp_fusion), kind=kCustom, calls=%fused_computation | custom fusion | bytes 12288 | tf_op jit(solution)/shard_map/jit(_take)/gather | solution.py:44
  15.7 0.1 gather.13
  15.8 0.0 copy-done.1
  15.8 0.0 copy-done.2
  15.8 0.1 compare_select_fusion.5
  15.9 0.6 pad_add_fusion
  16.5 7.3 %all-to-all-start = ((s32[32,1,64]{2,1,0:T(1,128)}), s32[32,1,64]{2,1,0:T(1,128)S(1)}, u32[]{:S(2)}, u32[]{:S(2)}) async-start(s32[32,1,64]{2,1,0:T(1,128)} %bitcast.2), calls=%async_computation | async-start | bytes 32768 | tf_op jit(solution)/shard_map/all_to_all | solution.py:59
  23.8 0.1 reshape.547
  23.9 0.1 broadcast_compare_fusion.1
  24.0 3.7 %concatenate.7 = f32[8256,128]{1,0:T(8,128)} pad(f32[8192,128]{1,0:T(8,128)} %param.7, f32[]{:T(128)} %constant.82.clone.1), padding=0_64x0_0 | pad | bytes 8421380 | tf_op jit(solution)/shard_map/concatenate | solution.py:38
  27.7 0.0 copy-start
  27.7 5.0 %gather_fusion.1 = f32[1024,128]{1,0:T(8,128)S(1)} fusion(f32[8256,128]{1,0:T(8,128)} %concatenate.7, s32[1024]{0:T(1024)S(1)} %broadcast_clamp_fusion), kind=kCustom, calls=%fused_computation.1 | custom fusion | bytes 1052672 | tf_op jit(solution)/shard_map/jit(_take)/gather | solution.py:43
  32.7 0.7 fusion.13
  33.5 1.1 pad_maximum_fusion
  34.6 0.0 all-to-all-done
  34.6 5.8 %all-to-all-start.1 = ((f32[32,64,128]{2,1,0:T(8,128)}), f32[32,64,128]{2,1,0:T(8,128)S(1)}, u32[]{:S(2)}, u32[]{:S(2)}) async-start(f32[32,64,128]{2,1,0:T(8,128)} %bitcast.4), calls=%async_computation.1 | async-start | bytes 2097152 | tf_op jit(solution)/shard_map/all_to_all | solution.py:58
  40.4 0.0 all-gather.2.cloned.1.call-start
  40.5 0.0 copy-done
  40.5 0.1 fusion.14
  40.6 0.1 select_n.222
  40.6 26.9 %all-to-all-done.1 = f32[32,64,128]{2,1,0:T(8,128)S(1)} async-done(((f32[32,64,128]{2,1,0:T(8,128)}), f32[32,64,128]{2,1,0:T(8,128)S(1)}, u32[]{:S(2)}, u32[]{:S(2)}) %all-to-all-start.1) | async-done | bytes 1048608 | tf_op jit(solution)/shard_map/all_to_all | solution.py:58
  67.6 0.0 copy-start.3
  67.6 8.6 %fusion.10 = f32[2048,128]{1,0:T(8,128)} fusion(f32[2048,128]{1,0:T(8,128)S(1)} %bitcast.20, s32[2048]{0:T(1024)S(1)} %select_n.222), kind=kOutput, calls=%fused_computation.12 | convolution fusion | flops 6446645248 | bytes 2105344 | tf_op jit(solution)/shard_map/while/body/eval_jaxpr/dot_general | solution.py:21
  76.1 0.0 all-gather.2.cloned.1.call-update
  76.2 0.2 reduce-scatter.2.cloned.1.call-start
  76.4 0.0 copy-done.3
  76.4 34.5 %while.3 = (s32[]{:T(128)}, f32[2048,128]{1,0:T(8,128)S(1)}, s32[2048]{0:T(1024)S(1)}, s32[4,2048]{1,0:T(4,128)S(1)}, f32[4,2048,128]{2,1,0:T(8,128)}, /*index=5*/s32[]{:T(128)}, s32[]{:T(128)}) while((s32[]{:T(128)}, f32[2048,128]{1,0:T(8,128)S(1)}, s32[2048]{0:T(1024)S(1)}, s32[4,2048]{1,0:T(4,128)S(1)}, ...), condition=%wide.region_1.2_spmd.clone, body=%wide.region_0.1_spmd.clone.sunk | while | flops 6447169536 | bytes 3178599 | solution.py:27
  76.4 8.6 %fusion.34 = f32[2048,128]{1,0:T(8,128)S(1)} fusion(s32[2048]{0:T(1024)S(1)} %bitcast.21, s32[2048]{0:T(1024)S(1)} %get-tuple-element.128, f32[2048,128]{1,0:T(8,128)S(1)} %get-tuple-element.120, f32[4,2048,128]{2,1,0:T(8,128)} %get-tuple-element.130, s32[]{:T(128)S(6)} %copy.9, pred[]{:T(512)S(6)} %compare.29), kind=kOutput, calls=%fused_computation.6.clone.1 | convolution fusion | flops 6447169536 | bytes 3162117 | tf_op jit(solution)/shard_map/while/body/eval_jaxpr/dot_general | solution.py:21
  85.1 8.6 %fusion.34 = f32[2048,128]{1,0:T(8,128)S(1)} fusion(s32[2048]{0:T(1024)S(1)} %bitcast.21, s32[2048]{0:T(1024)S(1)} %get-tuple-element.128, f32[2048,128]{1,0:T(8,128)S(1)} %get-tuple-element.120, f32[4,2048,128]{2,1,0:T(8,128)} %get-tuple-element.130, s32[]{:T(128)S(6)} %copy.9, pred[]{:T(512)S(6)} %compare.29), kind=kOutput, calls=%fused_computation.6.clone.1 | convolution fusion | flops 6447169536 | bytes 3162117 | tf_op jit(solution)/shard_map/while/body/eval_jaxpr/dot_general | solution.py:21
  93.7 8.6 %fusion.34 = f32[2048,128]{1,0:T(8,128)S(1)} fusion(s32[2048]{0:T(1024)S(1)} %bitcast.21, s32[2048]{0:T(1024)S(1)} %get-tuple-element.128, f32[2048,128]{1,0:T(8,128)S(1)} %get-tuple-element.120, f32[4,2048,128]{2,1,0:T(8,128)} %get-tuple-element.130, s32[]{:T(128)S(6)} %copy.9, pred[]{:T(512)S(6)} %compare.29), kind=kOutput, calls=%fused_computation.6.clone.1 | convolution fusion | flops 6447169536 | bytes 3162117 | tf_op jit(solution)/shard_map/while/body/eval_jaxpr/dot_general | solution.py:21
  102.3 8.6 %fusion.34 = f32[2048,128]{1,0:T(8,128)S(1)} fusion(s32[2048]{0:T(1024)S(1)} %bitcast.21, s32[2048]{0:T(1024)S(1)} %get-tuple-element.128, f32[2048,128]{1,0:T(8,128)S(1)} %get-tuple-element.120, f32[4,2048,128]{2,1,0:T(8,128)} %get-tuple-element.130, s32[]{:T(128)S(6)} %copy.9, pred[]{:T(512)S(6)} %compare.29), kind=kOutput, calls=%fused_computation.6.clone.1 | convolution fusion | flops 6447169536 | bytes 3162117 | tf_op jit(solution)/shard_map/while/body/eval_jaxpr/dot_general | solution.py:21
  110.9 0.9 collective-permute-start
  111.9 23.7 %collective-permute-done = f32[2048,128]{1,0:T(8,128)S(1)} collective-permute-done((f32[2048,128]{1,0:T(8,128)S(1)}, f32[2048,128]{1,0:T(8,128)S(1)}, u32[]{:S(2)}, u32[]{:S(2)}) %collective-permute-start) | collective-permute-done | bytes 1048608 | tf_op jit(solution)/shard_map/ppermute | solution.py:69
  135.5 1.1 add.141
  136.6 0.0 reduce-scatter.2.cloned.1.call-update
  136.6 0.0 all-gather.2.cloned.1.call-done
  136.7 55.3 %reduce-scatter.2.cloned.1.call-done = f32[128,128]{1,0:T(8,128)} async-done(((f32[2048,128]{1,0:T(8,128)}), f32[128,128]{1,0:T(8,128)}) %reduce-scatter.2.cloned.1.call-update) | async-done | bytes 65552 | tf_op jit(solution)/shard_map/reduce_scatter | solution.py:70
  192.0 3.0 %copy.14 = f32[4096,128]{1,0:T(8,128)} copy(f32[4096,128]{1,0:T(8,128)} %all-gather.2.cloned.1.call-done) | data formatting | bytes 4194304
  (9 shorter events, 0.1 us)
Async XLA Ops:
  9.6 6.2 %copy-start.1 = (s32[1,16]{1,0:T(1,128)S(1)}, s32[1,16]{1,0:T(1,128)}, u32[]{:S(2)}) copy-start(s32[1,16]{1,0:T(1,128)} %param.10) | copy-start | bytes 196
  9.6 6.2 %copy-start.2 = (s32[1,16]{1,0:T(1,128)S(1)}, s32[1,16]{1,0:T(1,128)}, u32[]{:S(2)}) copy-start(s32[1,16]{1,0:T(1,128)} %param.11) | copy-start | bytes 196
  16.5 18.0 %all-to-all-start = ((s32[32,1,64]{2,1,0:T(1,128)}), s32[32,1,64]{2,1,0:T(1,128)S(1)}, u32[]{:S(2)}, u32[]{:S(2)}) async-start(s32[32,1,64]{2,1,0:T(1,128)} %bitcast.2), calls=%async_computation | async-start | bytes 32768 | tf_op jit(solution)/shard_map/all_to_all | solution.py:59
  27.7 12.7 %copy-start = (s32[8192]{0:T(1024)S(1)}, s32[8192]{0:T(1024)}, u32[]{:S(2)}) copy-start(s32[8192]{0:T(1024)} %param.8) | copy-start | bytes 98308
  34.6 33.0 %all-to-all-start.1 = ((f32[32,64,128]{2,1,0:T(8,128)}), f32[32,64,128]{2,1,0:T(8,128)S(1)}, u32[]{:S(2)}, u32[]{:S(2)}) async-start(f32[32,64,128]{2,1,0:T(8,128)} %bitcast.4), calls=%async_computation.1 | async-start | bytes 2097152 | tf_op jit(solution)/shard_map/all_to_all | solution.py:58
  40.4 96.3 %all-gather.2.cloned.1.call-start = ((), (), s32[]{:S(2)}) async-start(), calls=%async_computation.3 | async-start | bytes 3145728 | tf_op jit(solution)/shard_map/all_gather | solution.py:67
  67.6 8.8 %copy-start.3 = (s32[2048]{0:T(1024)S(1)}, s32[2048]{0:T(1024)}, u32[]{:S(2)}) copy-start(s32[2048]{0:T(1024)} %param.9) | copy-start | bytes 24580
  76.2 115.8 %reduce-scatter.2.cloned.1.call-start = ((), (), s32[]{:S(2)}) async-start(), calls=%async_computation.4 | async-start | bytes 1114112 | tf_op jit(solution)/shard_map/reduce_scatter | solution.py:70
  110.9 24.6 %collective-permute-start = (f32[2048,128]{1,0:T(8,128)S(1)}, f32[2048,128]{1,0:T(8,128)S(1)}, u32[]{:S(2)}, u32[]{:S(2)}) collective-permute-start(f32[2048,128]{1,0:T(8,128)S(1)} %get-tuple-element.44), channel_id=1, source_target_pairs={{0,16},{16,0},{1,17},{17,1},{2,18},{18,2},{3,19},{19,3},{4,20},{20... | collective-permute-start | bytes 3145736 | tf_op jit(solution)/shard_map/ppermute | solution.py:69
Sparse Core Ops, SparseCore 0:
  76.3 30.3 all-gather.1
Sparse Core Ops, SparseCore 1:
  136.7 55.2 reduce-scatter.1
